TPU v7x, 64 devices: a 2x2x8 block of a 4x4x8 slice. The times are simulated.
64 devices in a mesh: dp: 8 (over x, y, core), sp: 8 (over z).
Axes of the slice: x: 2, y: 2, z: 8, core: 2. Of those that a mesh axis runs over, the one named last changes fastest.
The devices are a block of a 4x4x8 slice.
Arguments:
- q: bfloat16 [256, 4, 256], P('dp'), parts along dimension 0
- k: bfloat16 [256, 8192, 1, 256], P('dp', 'sp'), parts along dimension 0
- v: bfloat16 [256, 8192, 1, 256], P('dp', 'sp'), parts along dimension 0
Outputs:
- q: bfloat16 [256, 4, 256], P('dp'), parts along dimension 0
There are 8 independent parts. A program takes and returns all parts, laid end to end along the dimension named above; each array names one.
All inputs are finite; a program needn't handle non-finite values.
Results may differ from a plain program's by a relative error of at most 0.012.
Values are sent between devices in bfloat16 or wider.
A program may use at most 768 MiB of HBM per device.

v0:
```python
import jax
import jax.numpy as jnp
from jax import lax
from jax.sharding import PartitionSpec as P


def einsum(form, a, b):
    return jnp.einsum(form, a.astype(jnp.float32), b.astype(jnp.float32))


def part_of(q, k, v):
    grouped = q.reshape(q.shape[0], k.shape[2], -1, q.shape[2])
    scores = einsum("bgsd,bugd->bgsu", grouped, k) * q.shape[2] ** -0.5
    high = jnp.max(scores, -1, keepdims=True)
    weights = jnp.exp(scores - high)
    seen = einsum("bgsu,bugd->bgsd", weights.astype(jnp.bfloat16), v)
    return jnp.concatenate([seen, jnp.sum(weights, -1, keepdims=True), high], -1)


def together(parts):
    seen, total, high = parts[..., :-2], parts[..., -2:-1], parts[..., -1:]
    scale = jnp.exp(high - jnp.max(high, 0))
    return (jnp.sum(seen * scale, 0) / jnp.sum(total * scale, 0)).astype(jnp.bfloat16)


def solution(mesh):
    def step(q, k, v):
        return together(lax.all_gather(part_of(q, k, v), "sp")).reshape(q.shape)

    return jax.shard_map(
        step,
        mesh=mesh,
        in_specs=(P("dp", None, None), P("dp", "sp", None, None), P("dp", "sp", None, None)),
        out_specs=P("dp", None, None),
        check_vma=False,
    )
```

profile of v0, /device:TPU:22, one launch (start us, length us, event | category | flops | bytes accessed | tf_op | source)
XLA Modules:
  0.0 78.0 jit_solution(4212930165170867379)
XLA Ops:
  6.5 0.0 copy-start
  6.6 0.0 all-gather.3.cloned.1.call-start
  6.6 0.8 %copy-done = bf16[32,4,256]{2,1,0:T(4,128)(2,1)S(1)} copy-done((bf16[32,4,256]{2,1,0:T(4,128)(2,1)S(1)}, bf16[32,4,256]{2,1,0:T(4,128)(2,1)}, u32[]{:S(2)}) %copy-start) | copy-done | bytes 65560
  7.4 10.3 %fusion.17 = (f32[32,4]{1,0:T(8,128)S(1)}, f32[32,4,1024]{2,1,0:T(4,128)S(1)}) fusion(bf16[32,4,256]{2,1,0:T(4,128)(2,1)S(1)} %copy-done, bf16[32,1024,1,256]{3,1,2,0:T(8,128)(2,1)} %param.4), kind=kOutput, calls=%fused_computation.19 | convolution fusion | flops 67370880 | bytes 17367552 | tf_op jit(solution)/shard_map/bgsd,bugd->bgsu/dot_general | solution.py:8
  17.7 0.3 fusion.13
  18.0 8.1 %fusion.7 = f32[32,1,4,256]{3,2,0,1:T(4,128)S(1)} fusion(bf16[32,1024,1,256]{3,1,2,0:T(8,128)(2,1)} %param.5, f32[32,4,1024]{2,1,0:T(4,128)S(1)} %get-tuple-element.8, f32[32,4]{1,0:T(8,128)S(1)} %get-tuple-element.7), kind=kOutput, calls=%fused_computation.5 | convolution fusion | flops 67371008 | bytes 17433088 | tf_op jit(solution)/shard_map/bgsu,bugd->bgsd/dot_general | solution.py:8
  26.1 0.3 copy.30
  26.4 0.3 copy.31
  26.7 0.8 maximum_bitcast_fusion
  27.5 0.1 all-gather.3.cloned.1.call-update
  27.6 40.3 %all-gather.3.cloned.1.call-done = f32[256,1,4,258]{3,2,1,0:T(4,128)} async-done(((f32[32,1,4,258]{3,2,1,0:T(4,128)}), f32[256,1,4,258]{3,2,1,0:T(4,128)}) %all-gather.3.cloned.1.call-update) | async-done | bytes 1056784 | tf_op jit(solution)/shard_map/all_gather | solution.py:28
  67.9 1.5 %copy.33 = f32[256,1,4,258]{3,0,2,1:T(8,128)S(1)} copy(f32[256,1,4,258]{3,2,1,0:T(4,128)} %all-gather.3.cloned.1.call-done) | data formatting | bytes 2113536 | tf_op jit(solution)/shard_map/all_gather | solution.py:28
  69.4 0.3 slice_reduce_fusion
  69.7 0.5 fusion.11
  70.2 0.2 fusion.10
  70.4 0.1 divide_convert_fusion
  70.5 0.7 copy.35
Async XLA Ops:
  6.5 0.8 %copy-start = (bf16[32,4,256]{2,1,0:T(4,128)(2,1)S(1)}, bf16[32,4,256]{2,1,0:T(4,128)(2,1)}, u32[]{:S(2)}) copy-start(bf16[32,4,256]{2,1,0:T(4,128)(2,1)} %param.3) | copy-start | bytes 196612
  6.6 61.3 %all-gather.3.cloned.1.call-start = ((), (), s32[]{:S(2)}) async-start(), calls=%async_computation | async-start | bytes 1769472 | tf_op jit(solution)/shard_map/all_gather | solution.py:28
Sparse Core Ops, SparseCore 0:
  27.7 40.1 all-gather.2
where the time goes:
time: 78.2 us; the launch traced here: 78 us
  waiting for transfers between devices  40.4 us (52%)
  matrix products  18.4 us (24%)
  between operations  13.4 us (17%)
  local copies, waits for them, and re-layouts  3.65 us (5%)
  other arithmetic  2.15 us (3%)
    all_gather x1, waiting for transfers between devices, step(): return together(lax.all_gather(part_of(q, k, v), 'sp')).reshape(q.shape)  40.3 us
    dot_general x2, matrix products, einsum(): return jnp.einsum(form, a.astype(jnp.float32), b.astype(jnp.float32))  18.4 us
  transfers between devices with their start and end apart: 1, of which 1 were waited for; matrix products, arithmetic and copies ran while one was open for 0% of the time, Pallas kernels for 0%

commit v1 on v0

v1 whole, which is shorter than its diff:
```python
import functools

import jax
import jax.numpy as jnp
from jax import lax
from jax.experimental import pallas as pl
from jax.experimental.pallas import tpu as pltpu
from jax.sharding import PartitionSpec as P

MESH = pl.DeviceIdType.MESH


def offset_of(step, n):
    return n // 2 + (step // 2 if step % 2 == 0 else -(step + 1) // 2)


def kernel(n, q_ref, k_hbm, v_hbm, o_ref, kbuf, vbuf, q_all, part, stat, part_in, stat_in, k_sem, v_sem, send_sem, recv_sem, out_send, out_recv):
    me = lax.axis_index("sp")
    sequences, heads, head = q_ref.shape
    each = sequences // n
    rows = each * heads
    owners = [lax.rem(me + offset_of(step, n), n) for step in range(n)]

    def fetch(step, j):
        at = owners[step] * each + j
        slot = step * each + j
        return (
            pltpu.make_async_copy(k_hbm.at[at], kbuf.at[slot], k_sem.at[slot]),
            pltpu.make_async_copy(v_hbm.at[at], vbuf.at[slot], v_sem.at[slot]),
        )

    for j in range(each):
        fetch(0, j)[0].start()
    for step in range(n):
        if step + 1 < n:
            for j in range(each):
                fetch(step + 1, j)[0].start()
        for j in range(each):
            fetch(step, j)[1].start()

    barrier = pltpu.get_barrier_semaphore()
    for d in range(1, n):
        pl.semaphore_signal(barrier, inc=1, device_id={"sp": lax.rem(me + d, n)}, device_id_type=MESH)

    for g in range(n):
        q_all[g] = jnp.concatenate([q_ref[g * each + j].astype(jnp.float32) for j in range(each)], 0).astype(jnp.bfloat16)

    row = lax.broadcasted_iota(jnp.int32, (rows, 1), 0) // heads
    lane = lax.broadcasted_iota(jnp.int32, (rows, 128), 1)

    def scores_of(step):
        q = q_all[owners[step]]
        scores = None
        for j in range(each):
            fetch(step, j)[0].wait()
            s = lax.dot_general(q, kbuf[step * each + j], (((1,), (1,)), ((), ())), preferred_element_type=jnp.float32)
            scores = s if scores is None else jnp.where(row == j, s, scores)
        return scores * head**-0.5

    def send(step):
        d = offset_of(step, n)
        peer = {"sp": owners[step]}
        return (
            pltpu.make_async_remote_copy(part.at[d], part_in.at[d], send_sem.at[d, 0], recv_sem.at[d, 0], device_id=peer, device_id_type=MESH),
            pltpu.make_async_remote_copy(stat.at[d], stat_in.at[d], send_sem.at[d, 1], recv_sem.at[d, 1], device_id=peer, device_id_type=MESH),
        )

    scores = scores_of(0)
    for step in range(n):
        following = scores_of(step + 1) if step + 1 < n else None
        high = jnp.max(scores, -1, keepdims=True)
        weights = jnp.exp(scores - high)
        total = jnp.sum(weights, -1, keepdims=True)
        weights = weights.astype(jnp.bfloat16)
        seen = None
        for j in range(each):
            fetch(step, j)[1].wait()
            s = jnp.dot(weights, vbuf[step * each + j], preferred_element_type=jnp.float32)
            seen = s if seen is None else jnp.where(row == j, s, seen)
        if step + 1 < n:
            d = offset_of(step, n)
            part[d] = seen.astype(jnp.bfloat16)
            stat[d] = jnp.where(lane < 64, total, high)
            if step == 0:
                pl.semaphore_wait(barrier, n - 1)
            for copy in send(step):
                copy.start()
        scores = following

    highs, totals = [high], [total]
    for d in range(1, n):
        for copy in send([offset_of(s, n) for s in range(n)].index(d)):
            copy.wait_recv()
        highs.append(stat_in[d][:, 64:65])
        totals.append(stat_in[d][:, 0:1])
    top = functools.reduce(jnp.maximum, highs)
    scales = [jnp.exp(h - top) for h in highs]
    whole = sum(t * s for t, s in zip(totals, scales))
    result = seen * scales[0]
    for d in range(1, n):
        result += part_in[d].astype(jnp.float32) * scales[d]
    o_ref[me] = (result / whole).astype(o_ref.dtype)

    def spread(d):
        return pltpu.make_async_remote_copy(
            o_ref.at[me], o_ref.at[me], out_send.at[d], out_recv.at[d], device_id={"sp": lax.rem(me + d, n)}, device_id_type=MESH
        )

    order = [offset_of(step, n) for step in range(n - 1)]
    for d in order:
        spread(d).start()
    for step in range(n - 1):
        for copy in send(step):
            copy.wait_send()
    for d in order:
        spread(d).wait_send()
    for d in order:
        source = lax.rem(me - d + n, n)
        pltpu.make_async_remote_copy(
            o_ref.at[source], o_ref.at[source], out_send.at[d], out_recv.at[d], device_id={"sp": lax.rem(me + d, n)}, device_id_type=MESH
        ).wait_recv()


def attend(n, q, k, v):
    sequences, heads, head = q.shape
    tokens = k.shape[1]
    rows = sequences // n * heads
    out = pl.pallas_call(
        functools.partial(kernel, n),
        out_shape=jax.ShapeDtypeStruct((n, rows, head), q.dtype),
        in_specs=[
            pl.BlockSpec(memory_space=pltpu.VMEM),
            pl.BlockSpec(memory_space=pl.ANY),
            pl.BlockSpec(memory_space=pl.ANY),
        ],
        out_specs=pl.BlockSpec(memory_space=pltpu.VMEM),
        scratch_shapes=[
            pltpu.VMEM((sequences, tokens, head), k.dtype),
            pltpu.VMEM((sequences, tokens, head), v.dtype),
            pltpu.VMEM((n, rows, head), q.dtype),
            pltpu.VMEM((n, rows, head), jnp.bfloat16),
            pltpu.VMEM((n, rows, 128), jnp.float32),
            pltpu.VMEM((n, rows, head), jnp.bfloat16),
            pltpu.VMEM((n, rows, 128), jnp.float32),
            pltpu.SemaphoreType.DMA((sequences,)),
            pltpu.SemaphoreType.DMA((sequences,)),
            pltpu.SemaphoreType.DMA((n, 2)),
            pltpu.SemaphoreType.DMA((n, 2)),
            pltpu.SemaphoreType.DMA((n,)),
            pltpu.SemaphoreType.DMA((n,)),
        ],
        compiler_params=pltpu.CompilerParams(collective_id=0, has_side_effects=True, vmem_limit_bytes=56 * 2**20),
    )(q, k.reshape(sequences, tokens, head), v.reshape(sequences, tokens, head))
    return out.reshape(q.shape)


def solution(mesh):
    return jax.shard_map(
        functools.partial(attend, mesh.shape["sp"]),
        mesh=mesh,
        in_specs=(P("dp", None, None), P("dp", "sp", None, None), P("dp", "sp", None, None)),
        out_specs=P("dp", None, None),
        check_vma=False,
    )
```

time: 78.2 us -> 33.6 us (0.43)
  waiting for transfers between devices: 40.4 us -> 0 us
  Pallas kernels: 0 us -> 32 us
  matrix products: 18.4 us -> 0 us
  between operations: 13.4 us -> 0.01 us
  local copies, waits for them, and re-layouts: 3.65 us -> 1.49 us
  other arithmetic: 2.15 us -> 0 us
    all_gather x1 -> x0, waiting for transfers between devices: 40.3 us -> none  [step(): return together(lax.all_gather(part_of(q, k, v), 'sp')).reshape(q.shape)]
    pallas_call x0 -> x1, Pallas kernels: none -> 32 us  [attend(): pl.pallas_call(functools.partial(kernel, n), out_shape=jax.ShapeDtypeStru...]
    dot_general x2 -> x0, matrix products: 18.4 us -> none  [einsum(): return jnp.einsum(form, a.astype(jnp.float32), b.astype(jnp.float32))]
    all_gather x1 -> x0, local copies, waits for them, and re-layouts: 1.51 us -> none  [step(): return together(lax.all_gather(part_of(q, k, v), 'sp')).reshape(q.shape)]
    reshape x0 -> x1, local copies, waits for them, and re-layouts: none -> 1.49 us  [attend(): return out.reshape(q.shape)]
    reduce_sum x3 -> x0, other arithmetic: 1 us -> none  [the longest x1 0.46 us: together(): jnp.sum(total * scale, 0)]
    unnamed x2 -> x0, local copies, waits for them, and re-layouts: 0.84 us -> none
  transfers between devices with their start and end apart: 1 -> 0, of which waited for: 1 -> 0; matrix products, arithmetic and copies ran while one was open for 0% -> 0% of each run, Pallas kernels for 0% -> 0%
where the time goes in v1:
time: 33.6 us; the launch traced here: 33.5 us
  Pallas kernels  32 us (95%)
  local copies, waits for them, and re-layouts  1.49 us (4%)
    pallas_call x1, Pallas kernels, attend(): pl.pallas_call(functools.partial(kernel, n), out_shape=jax.ShapeDtypeStru...  32 us
    reshape x1, local copies, waits for them, and re-layouts, attend(): return out.reshape(q.shape)  1.49 us

profile of v1, /device:TPU:22, one launch (start us, length us, event | category | flops | bytes accessed | tf_op | source)
XLA Modules:
  0.0 33.5 jit_solution(1266067017180029875)
XLA Ops:
  0.0 32.0 %shard_map.37 = bf16[8,16,256]{2,1,0:T(8,128)(2,1)} custom-call(bf16[32,4,256]{2,1,0:T(4,128)(2,1)} %q_ref.1, bf16[32,1024,256]{2,1,0:T(8,128)(2,1)} %bitcast.2, bf16[32,1024,256]{2,1,0:T(8,128)(2,1)} %bitcast.3), custom_call_target="tpu_custom_call" | custom-call | tf_op jit(solution)/shard_map/pallas_call | solution.py:128
  32.0 1.5 %reshape.11 = bf16[32,4,256]{2,1,0:T(4,128)(2,1)} reshape(bf16[8,16,256]{2,1,0:T(8,128)(2,1)} %shard_map.37) | data formatting | bytes 131072 | tf_op jit(solution)/shard_map/reshape | solution.py:154

commit v2 on v1

v2 whole, which is shorter than its diff:
```python
import functools

import jax
import jax.numpy as jnp
from jax import lax
from jax.experimental import pallas as pl
from jax.experimental.pallas import tpu as pltpu
from jax.sharding import PartitionSpec as P

MESH = pl.DeviceIdType.MESH
TILE = 256
UNITS = 2


def offset_of(step, n):
    if isinstance(step, int):
        return n // 2 + (step // 2 if step % 2 == 0 else -(step + 1) // 2)
    return n // 2 + jnp.where(step % 2 == 0, step // 2, -((step + 1) // 2))


def kernel(n, q_ref, k_hbm, v_hbm, o_ref, *refs):
    sequences, heads, head = q_ref.shape
    each = sequences // n
    tiles = k_hbm.shape[1] // TILE
    deep = tiles // UNITS
    body(n, q_ref, k_hbm, v_hbm, o_ref, *refs, None)


def body(
    n, q_ref, k_hbm, v_hbm, o_ref, kbuf, vbuf, q_all, part, stat, part_in, stat_in, k_sem, v_sem, send_sem, recv_sem, out_send, out_recv, accs
):
    me = lax.axis_index("sp")
    sequences, heads, head = q_ref.shape
    each = sequences // n
    rows = each * heads
    tiles = kbuf.shape[1] // TILE
    deep = tiles // UNITS

    def owner(step):
        return lax.rem(me + offset_of(step, n), n)

    def fetch_k(step, j):
        slot = step * each + j
        return pltpu.make_async_copy(k_hbm.at[owner(step) * each + j], kbuf.at[slot], k_sem.at[slot])

    def fetch_v(step, j):
        slot = step * each + j
        return pltpu.make_async_copy(v_hbm.at[owner(step) * each + j], vbuf.at[slot], v_sem.at[slot])

    def start(fetch, step):
        for j in range(each):
            fetch(step, j).start()

    start(fetch_k, 0)

    @pl.loop(0, n - 1)
    def _(step):
        start(fetch_k, step + 1)
        start(fetch_v, step)

    start(fetch_v, n - 1)

    barrier = pltpu.get_barrier_semaphore()
    for d in range(1, n):
        pl.semaphore_signal(barrier, inc=1, device_id={"sp": lax.rem(me + d, n)}, device_id_type=MESH)

    for g in range(n):
        q_all[g] = jnp.concatenate([q_ref[g * each + j].astype(jnp.float32) for j in range(each)], 0).astype(jnp.bfloat16)

    row = lax.broadcasted_iota(jnp.int32, (rows, 1), 0) // heads
    lane = lax.broadcasted_iota(jnp.int32, (rows, 128), 1)

    def pick(values):
        out = values[0]
        for j in range(1, each):
            out = jnp.where(row == j, values[j], out)
        return out

    def multiply_k(step):
        q = q_all[owner(step)]
        out = {}
        for j in range(each):
            fetch_k(step, j).wait()
        for j in range(each):
            for t in range(deep):
                for u in range(UNITS):
                    at = (u * deep + t) * TILE
                    out[u, j, t] = lax.dot_general(
                        q, kbuf[step * each + j, at : at + TILE, :], (((1,), (1,)), ((), ())), preferred_element_type=jnp.float32
                    )
        return out

    def take_scores(out):
        return [
            pick([out[u, j, t] for j in range(each)]) * head**-0.5 for u in range(UNITS) for t in range(deep)
        ]

    def soften(scores):
        high = jnp.max(functools.reduce(jnp.maximum, scores), -1, keepdims=True)
        weights = [jnp.exp(s - high) for s in scores]
        total = jnp.sum(functools.reduce(jnp.add, weights), -1, keepdims=True)
        return high, total, [w.astype(jnp.bfloat16) for w in weights]

    def multiply_v(step, weights, split):
        out = {}
        if not split:
            for j in range(each):
                fetch_v(step, j).wait()
        for j in range(each):
            if split:
                fetch_v(step, j).wait()
            for t in range(deep):
                for u in range(UNITS):
                    at = (u * deep + t) * TILE
                    s = jnp.dot(weights[u * deep + t], vbuf[step * each + j, at : at + TILE, :], preferred_element_type=jnp.float32)
                    out[j] = out[j] + s if j in out else s
        return out

    def take_seen(out):
        return pick([out[j] for j in range(each)])

    def send(step):
        d = offset_of(step, n)
        peer = {"sp": owner(step)}
        return (
            pltpu.make_async_remote_copy(part.at[step], part_in.at[d], send_sem.at[step, 0], recv_sem.at[d, 0], device_id=peer, device_id_type=MESH),
            pltpu.make_async_remote_copy(stat.at[step], stat_in.at[d], send_sem.at[step, 1], recv_sem.at[d, 1], device_id=peer, device_id_type=MESH),
        )

    def turn(step, scores):
        out = multiply_k(step + 1)
        high, total, weights = soften(scores)
        seen = multiply_v(step, weights, False)
        following = take_scores(out)
        part[step] = take_seen(seen).astype(jnp.bfloat16)
        stat[step] = jnp.where(lane < 64, total, high)
        return following

    def dispatch(step):
        for copy in send(step):
            copy.start()

    scores = turn(0, take_scores(multiply_k(0)))
    pl.semaphore_wait(barrier, n - 1)
    dispatch(0)

    def loop(step, scores):
        scores = turn(step, scores)
        dispatch(step)
        return scores

    scores = lax.fori_loop(1, n - 1, loop, scores)
    high, total, weights = soften(scores)
    seen = take_seen(multiply_v(n - 1, weights, True))

    highs, totals = [high], [total]
    for step in range(n - 1):
        d = offset_of(step, n)
        for copy in send(step):
            copy.wait_recv()
        highs.append(stat_in[d][:, 64:65])
        totals.append(stat_in[d][:, 0:1])
    top = functools.reduce(jnp.maximum, highs)
    scales = [jnp.exp(h - top) for h in highs]
    whole = sum(t * s for t, s in zip(totals, scales))
    result = seen * scales[0]
    for step in range(n - 1):
        result += part_in[offset_of(step, n)].astype(jnp.float32) * scales[step + 1]
    o_ref[me] = (result / whole).astype(o_ref.dtype)

    def spread(d, block):
        return pltpu.make_async_remote_copy(
            o_ref.at[block], o_ref.at[block], out_send.at[d], out_recv.at[d], device_id={"sp": lax.rem(me + d, n)}, device_id_type=MESH
        )

    order = [offset_of(step, n) for step in range(n - 1)]
    for d in order:
        spread(d, me).start()
    for step in range(n - 1):
        for copy in send(step):
            copy.wait_send()
    for d in order:
        spread(d, me).wait_send()
    for d in order:
        spread(d, lax.rem(me - d + n, n)).wait_recv()


def attend(n, q, k, v):
    sequences, heads, head = q.shape
    tokens = k.shape[1]
    rows = sequences // n * heads
    out = pl.pallas_call(
        functools.partial(kernel, n),
        out_shape=jax.ShapeDtypeStruct((n, rows, head), q.dtype),
        in_specs=[
            pl.BlockSpec(memory_space=pltpu.VMEM),
            pl.BlockSpec(memory_space=pl.ANY),
            pl.BlockSpec(memory_space=pl.ANY),
        ],
        out_specs=pl.BlockSpec(memory_space=pltpu.VMEM),
        scratch_shapes=[
            pltpu.VMEM((sequences, tokens, head), k.dtype),
            pltpu.VMEM((sequences, tokens, head), v.dtype),
            pltpu.VMEM((n, rows, head), q.dtype),
            pltpu.VMEM((n, rows, head), jnp.bfloat16),
            pltpu.VMEM((n, rows, 128), jnp.float32),
            pltpu.VMEM((n, rows, head), jnp.bfloat16),
            pltpu.VMEM((n, rows, 128), jnp.float32),
            pltpu.SemaphoreType.DMA((sequences,)),
            pltpu.SemaphoreType.DMA((sequences,)),
            pltpu.SemaphoreType.DMA((n, 2)),
            pltpu.SemaphoreType.DMA((n, 2)),
            pltpu.SemaphoreType.DMA((n,)),
            pltpu.SemaphoreType.DMA((n,)),
        ],
        compiler_params=pltpu.CompilerParams(collective_id=0, has_side_effects=True, vmem_limit_bytes=56 * 2**20),
    )(q, k.reshape(sequences, tokens, head), v.reshape(sequences, tokens, head))
    return out.reshape(q.shape)


def solution(mesh):
    return jax.shard_map(
        functools.partial(attend, mesh.shape["sp"]),
        mesh=mesh,
        in_specs=(P("dp", None, None), P("dp", "sp", None, None), P("dp", "sp", None, None)),
        out_specs=P("dp", None, None),
        check_vma=False,
    )
```

time: 33.6 us -> 27.8 us (0.83)
  Pallas kernels: 32 us -> 26.1 us
    pallas_call x1, Pallas kernels: 32 us -> 26.1 us  [attend(): pl.pallas_call(functools.partial(kernel, n), out_shape=jax.ShapeDtypeStru...]
where the time goes in v2:
time: 27.8 us; the launch traced here: 27.6 us
  Pallas kernels  26.1 us (94%)
  local copies, waits for them, and re-layouts  1.49 us (5%)
    pallas_call x1, Pallas kernels, attend(): pl.pallas_call(functools.partial(kernel, n), out_shape=jax.ShapeDtypeStru...  26.1 us
    reshape x1, local copies, waits for them, and re-layouts, attend(): return out.reshape(q.shape)  1.49 us

profile of v2, /device:TPU:22, one launch (start us, length us, event | category | flops | bytes accessed | tf_op | source)
XLA Modules:
  0.0 27.6 jit_solution(3524493504672548130)
XLA Ops:
  0.0 26.1 %shard_map.37 = bf16[8,16,256]{2,1,0:T(8,128)(2,1)} custom-call(bf16[32,4,256]{2,1,0:T(4,128)(2,1)} %q_ref.1, bf16[32,1024,256]{2,1,0:T(8,128)(2,1)} %bitcast.2, bf16[32,1024,256]{2,1,0:T(8,128)(2,1)} %bitcast.3), custom_call_target="tpu_custom_call" | custom-call | tf_op jit(solution)/shard_map/pallas_call | solution.py:192
  26.1 1.5 %reshape.11 = bf16[32,4,256]{2,1,0:T(4,128)(2,1)} reshape(bf16[8,16,256]{2,1,0:T(8,128)(2,1)} %shard_map.37) | data formatting | bytes 131072 | tf_op jit(solution)/shard_map/reshape | solution.py:218

commit v3 on v2

v3 whole, which is shorter than its diff:
```python
import functools

import jax
import jax.numpy as jnp
from jax import lax
from jax.experimental import pallas as pl
from jax.experimental.pallas import tpu as pltpu
from jax.sharding import PartitionSpec as P

MESH = pl.DeviceIdType.MESH
TILE = 256
AHEAD = 2


def offset_of(step, n):
    if isinstance(step, int):
        return n // 2 + (step // 2 if step % 2 == 0 else -(step + 1) // 2)
    return n // 2 + jnp.where(step % 2 == 0, step // 2, -((step + 1) // 2))


def kernel(
    n, q_hbm, k_hbm, v_hbm, o_ref, qbuf, kbuf, vbuf, q_all, s_all, w_all, sum_all, top_all, part, stat, part_in, stat_in,
    q_sem, k_sem, v_sem, last_sem, send_sem, recv_sem, out_send, out_recv,
):
    me = lax.axis_index("sp")
    sequences, heads, head = q_hbm.shape
    each = sequences // n
    rows = each * heads
    tiles = kbuf.shape[2] // TILE

    def owner(step):
        return lax.rem(me + offset_of(step, n), n)

    def run(step):
        return pl.ds(owner(step) * each, each)

    def fetch_k(step):
        return pltpu.make_async_copy(k_hbm.at[run(step)], kbuf.at[step], k_sem.at[step])

    def fetch_v(step):
        return pltpu.make_async_copy(v_hbm.at[run(step)], vbuf.at[step], v_sem.at[step])

    def fetch_last(j):
        return pltpu.make_async_copy(v_hbm.at[me * each + j], vbuf.at[n - 1, j], last_sem.at[j])

    def pieces(hbm, buf, sem, step):
        return [pltpu.make_async_copy(hbm.at[owner(step) * each + j], buf.at[step, j], sem.at[step]) for j in range(each)]

    def start_k(step):
        for piece in pieces(k_hbm, kbuf, k_sem, step):
            piece.start()

    def start_v(step):
        for piece in pieces(v_hbm, vbuf, v_sem, step):
            piece.start()

    fetch_q = pltpu.make_async_copy(q_hbm, qbuf, q_sem)
    start_k(0)
    fetch_q.start()

    for step in range(1, AHEAD):
        start_k(step)

    @pl.loop(0, n - AHEAD)
    def _(step):
        start_k(step + AHEAD)
        start_v(step)

    for step in range(n - AHEAD, n - 1):
        start_v(step)
    for j in range(each):
        fetch_last(j).start()

    barrier = pltpu.get_barrier_semaphore()
    for d in range(1, n):
        pl.semaphore_signal(barrier, inc=1, device_id={"sp": lax.rem(me + d, n)}, device_id_type=MESH)

    fetch_q.wait()
    for g in range(n):
        q_all[g] = jnp.concatenate([qbuf[g * each + j].astype(jnp.float32) for j in range(each)], 0).astype(jnp.bfloat16)

    row = lax.broadcasted_iota(jnp.int32, (rows, 1), 0) // heads
    lane = lax.broadcasted_iota(jnp.int32, (rows, 128), 1)

    def pick(values):
        out = values[0]
        for j in range(1, each):
            out = jnp.where(row == j, values[j], out)
        return out

    def span(t):
        return slice(t * TILE, (t + 1) * TILE)

    turns = [t + u * (tiles // 2) for t in range(tiles // 2) for u in range(2)]

    def score(step):
        q = q_all[owner(step)]
        out = {
            (j, t): lax.dot_general(q, kbuf[step, j, span(t), :], (((1,), (1,)), ((), ())), preferred_element_type=jnp.float32)
            for j in range(each)
            for t in turns
        }
        for t in range(tiles):
            s_all[step, t] = pick([out[j, t] for j in range(each)])

    def soften(step):
        scores = [s_all[step, t] * head**-0.5 for t in range(tiles)]
        high = jnp.max(functools.reduce(jnp.maximum, scores), -1, keepdims=True)
        weights = [jnp.exp(s - high) for s in scores]
        total = jnp.sum(functools.reduce(jnp.add, weights), -1, keepdims=True)
        for t in range(tiles):
            w_all[step, t] = weights[t].astype(jnp.bfloat16)
        stat[step] = jnp.where(lane < 64, total, high)

    def gather(step, split):
        out = []
        for j in range(each):
            if split:
                fetch_last(j).wait()
            dots = {t: jnp.dot(w_all[step, t], vbuf[step, j, span(t), :], preferred_element_type=jnp.float32) for t in turns}
            halves = [functools.reduce(jnp.add, [dots[t + u * (tiles // 2)] for t in range(tiles // 2)]) for u in range(2)]
            out.append(halves[0] + halves[1])
        return pick(out)

    def send(step):
        d = offset_of(step, n)
        peer = {"sp": owner(step)}
        return (
            pltpu.make_async_remote_copy(part.at[step], part_in.at[d], send_sem.at[step, 0], recv_sem.at[d, 0], device_id=peer, device_id_type=MESH),
            pltpu.make_async_remote_copy(stat.at[step], stat_in.at[d], send_sem.at[step, 1], recv_sem.at[d, 1], device_id=peer, device_id_type=MESH),
        )

    def dispatch(step):
        for copy in send(step):
            copy.start()

    @pl.loop(0, AHEAD)
    def _(step):
        fetch_k(step).wait()
        score(step)
        soften(step)

    @pl.loop(0, n - AHEAD)
    def _(step):
        fetch_k(step + AHEAD).wait()
        fetch_v(step).wait()
        score(step + AHEAD)
        part[step] = gather(step, False).astype(jnp.bfloat16)
        soften(step + AHEAD)

        @pl.when(step == 0)
        def _():
            pl.semaphore_wait(barrier, n - 1)

        dispatch(step)

    @pl.loop(n - AHEAD, n - 1)
    def _(step):
        fetch_v(step).wait()
        part[step] = gather(step, False).astype(jnp.bfloat16)
        dispatch(step)

    seen = gather(n - 1, True)
    high, total = stat[n - 1][:, 64:65], stat[n - 1][:, 0:1]

    def put(values):
        o_ref[me] = values.astype(o_ref.dtype)

    highs, totals = [high], [total]
    for step in range(n - 1):
        d = offset_of(step, n)
        for copy in send(step):
            copy.wait_recv()
        highs.append(stat_in[d][:, 64:65])
        totals.append(stat_in[d][:, 0:1])
    top = functools.reduce(jnp.maximum, highs)
    scales = [jnp.exp(h - top) for h in highs]
    whole = sum(t * s for t, s in zip(totals, scales))
    result = seen * scales[0]
    for step in range(n - 1):
        result += part_in[offset_of(step, n)].astype(jnp.float32) * scales[step + 1]
    put(result / whole)

    def spread(d, block):
        at = o_ref.at[block]
        return pltpu.make_async_remote_copy(
            at, at, out_send.at[d], out_recv.at[d], device_id={"sp": lax.rem(me + d, n)}, device_id_type=MESH
        )

    order = [offset_of(step, n) for step in range(n - 1)]
    for d in order:
        spread(d, me).start()
    for step in range(n - 1):
        for copy in send(step):
            copy.wait_send()
    for d in order:
        spread(d, me).wait_send()
    for d in order:
        spread(d, lax.rem(me - d + n, n)).wait_recv()


def attend(n, q, k, v):
    sequences, heads, head = q.shape
    tokens = k.shape[1]
    rows = sequences // n * heads
    tiles = tokens // TILE
    out = pl.pallas_call(
        functools.partial(kernel, n),
        out_shape=jax.ShapeDtypeStruct((n, rows, head), q.dtype),
        in_specs=[pl.BlockSpec(memory_space=pltpu.HBM)] * 3,
        out_specs=pl.BlockSpec(memory_space=pltpu.VMEM),
        scratch_shapes=[
            pltpu.VMEM(q.shape, q.dtype),
            pltpu.VMEM((n, sequences // n, tokens, head), k.dtype),
            pltpu.VMEM((n, sequences // n, tokens, head), v.dtype),
            pltpu.VMEM((n, rows, head), q.dtype),
            pltpu.VMEM((n, tiles, rows, TILE), jnp.float32),
            pltpu.VMEM((n, tiles, rows, TILE), jnp.bfloat16),
            pltpu.VMEM((n, rows, 128), jnp.float32),
            pltpu.VMEM((n, rows, 128), jnp.float32),
            pltpu.VMEM((n, rows, head), jnp.bfloat16),
            pltpu.VMEM((n, rows, 128), jnp.float32),
            pltpu.VMEM((n, rows, head), jnp.bfloat16),
            pltpu.VMEM((n, rows, 128), jnp.float32),
            pltpu.SemaphoreType.DMA,
            pltpu.SemaphoreType.DMA((n,)),
            pltpu.SemaphoreType.DMA((n,)),
            pltpu.SemaphoreType.DMA((sequences // n,)),
            pltpu.SemaphoreType.DMA((n, 2)),
            pltpu.SemaphoreType.DMA((n, 2)),
            pltpu.SemaphoreType.DMA((n,)),
            pltpu.SemaphoreType.DMA((n,)),
        ],
        compiler_params=pltpu.CompilerParams(collective_id=0, has_side_effects=True, vmem_limit_bytes=48 * 2**20),
    )(pltpu.with_memory_space_constraint(q, pltpu.HBM), k.reshape(sequences, tokens, head), v.reshape(sequences, tokens, head))
    return out.reshape(q.shape)


def solution(mesh):
    return jax.shard_map(
        functools.partial(attend, mesh.shape["sp"]),
        mesh=mesh,
        in_specs=(P("dp", None, None), P("dp", "sp", None, None), P("dp", "sp", None, None)),
        out_specs=P("dp", None, None),
        check_vma=False,
    )
```

time: 27.8 us -> 24.8 us (0.89)
  Pallas kernels: 26.1 us -> 24.1 us
  local copies, waits for them, and re-layouts: 1.49 us -> 0.65 us
    pallas_call x1, Pallas kernels: 26.1 us -> 24.1 us  [attend(): pl.pallas_call(functools.partial(kernel, n), out_shape=jax.ShapeDtypeStru...]
    reshape x1, local copies, waits for them, and re-layouts: 1.49 us -> 0.65 us  [attend(): return out.reshape(q.shape)]
where the time goes in v3:
time: 24.8 us; the launch traced here: 24.7 us
  Pallas kernels  24.1 us (97%)
  local copies, waits for them, and re-layouts  0.65 us (3%)
    pallas_call x1, Pallas kernels, attend(): pl.pallas_call(functools.partial(kernel, n), out_shape=jax.ShapeDtypeStru...  24.1 us
    reshape x1, local copies, waits for them, and re-layouts, attend(): return out.reshape(q.shape)  0.65 us

profile of v3, /device:TPU:22, one launch (start us, length us, event | category | flops | bytes accessed | tf_op | source)
XLA Modules:
  0.0 24.7 jit_solution(5766652175899803794)
XLA Ops:
  0.0 24.1 %shard_map.37 = bf16[8,16,256]{2,1,0:T(8,128)(2,1)S(1)} custom-call(bf16[32,4,256]{2,1,0:T(4,128)(2,1)} %q_hbm.1, bf16[32,1024,256]{2,1,0:T(8,128)(2,1)} %bitcast.2, bf16[32,1024,256]{2,1,0:T(8,128)(2,1)} %bitcast.3), custom_call_target="tpu_custom_call" | custom-call | tf_op jit(solution)/shard_map/pallas_call | solution.py:207
  24.1 0.7 %reshape.11 = bf16[32,4,256]{2,1,0:T(4,128)(2,1)} reshape(bf16[8,16,256]{2,1,0:T(8,128)(2,1)S(1)} %shard_map.37) | data formatting | bytes 131072 | tf_op jit(solution)/shard_map/reshape | solution.py:236

commit v4 on v3

--- a/solution.py
+++ b/solution.py
@@ -14,8 +14,8 @@
 
 def offset_of(step, n):
     if isinstance(step, int):
-        return n // 2 + (step // 2 if step % 2 == 0 else -(step + 1) // 2)
-    return n // 2 + jnp.where(step % 2 == 0, step // 2, -((step + 1) // 2))
+        return n // 2 + step if step < n // 2 else n - 1 - step
+    return jnp.where(step < n // 2, n // 2 + step, n - 1 - step)
 
 
 def kernel(

time: 24.8 us -> 24.6 us (level)
  Pallas kernels: 24.1 us -> 23.8 us
where the time goes in v4:
time: 24.6 us; the launch traced here: 24.5 us
  Pallas kernels  23.8 us (97%)
  local copies, waits for them, and re-layouts  0.65 us (3%)
    pallas_call x1, Pallas kernels, attend(): pl.pallas_call(functools.partial(kernel, n), out_shape=jax.ShapeDtypeStru...  23.8 us
    reshape x1, local copies, waits for them, and re-layouts, attend(): return out.reshape(q.shape)  0.65 us

profile of v4, /device:TPU:22, one launch (start us, length us, event | category | flops | bytes accessed | tf_op | source)
XLA Modules:
  0.0 24.5 jit_solution(15407681657056762054)
XLA Ops:
  0.0 23.8 %shard_map.37 = bf16[8,16,256]{2,1,0:T(8,128)(2,1)S(1)} custom-call(bf16[32,4,256]{2,1,0:T(4,128)(2,1)} %q_hbm.1, bf16[32,1024,256]{2,1,0:T(8,128)(2,1)} %bitcast.2, bf16[32,1024,256]{2,1,0:T(8,128)(2,1)} %bitcast.3), custom_call_target="tpu_custom_call" | custom-call | tf_op jit(solution)/shard_map/pallas_call | solution.py:207
  23.8 0.7 %reshape.11 = bf16[32,4,256]{2,1,0:T(4,128)(2,1)} reshape(bf16[8,16,256]{2,1,0:T(8,128)(2,1)S(1)} %shard_map.37) | data formatting | bytes 131072 | tf_op jit(solution)/shard_map/reshape | solution.py:236

commit v5 on v4

--- a/solution.py
+++ b/solution.py
@@ -20,7 +20,7 @@
 
 def kernel(
     n, q_hbm, k_hbm, v_hbm, o_ref, qbuf, kbuf, vbuf, q_all, s_all, w_all, sum_all, top_all, part, stat, part_in, stat_in,
-    q_sem, k_sem, v_sem, last_sem, send_sem, recv_sem, out_send, out_recv,
+    q_sem, k_sem, v_sem, send_sem, recv_sem, out_send, out_recv,
 ):
     me = lax.axis_index("sp")
     sequences, heads, head = q_hbm.shape
@@ -40,9 +40,6 @@
     def fetch_v(step):
         return pltpu.make_async_copy(v_hbm.at[run(step)], vbuf.at[step], v_sem.at[step])
 
-    def fetch_last(j):
-        return pltpu.make_async_copy(v_hbm.at[me * each + j], vbuf.at[n - 1, j], last_sem.at[j])
-
     def pieces(hbm, buf, sem, step):
         return [pltpu.make_async_copy(hbm.at[owner(step) * each + j], buf.at[step, j], sem.at[step]) for j in range(each)]
 
@@ -66,10 +63,8 @@
         start_k(step + AHEAD)
         start_v(step)
 
-    for step in range(n - AHEAD, n - 1):
+    for step in range(n - AHEAD, n):
         start_v(step)
-    for j in range(each):
-        fetch_last(j).start()
 
     barrier = pltpu.get_barrier_semaphore()
     for d in range(1, n):
@@ -112,11 +107,9 @@
             w_all[step, t] = weights[t].astype(jnp.bfloat16)
         stat[step] = jnp.where(lane < 64, total, high)
 
-    def gather(step, split):
+    def gather(step):
         out = []
         for j in range(each):
-            if split:
-                fetch_last(j).wait()
             dots = {t: jnp.dot(w_all[step, t], vbuf[step, j, span(t), :], preferred_element_type=jnp.float32) for t in turns}
             halves = [functools.reduce(jnp.add, [dots[t + u * (tiles // 2)] for t in range(tiles // 2)]) for u in range(2)]
             out.append(halves[0] + halves[1])
@@ -145,7 +138,7 @@
         fetch_k(step + AHEAD).wait()
         fetch_v(step).wait()
         score(step + AHEAD)
-        part[step] = gather(step, False).astype(jnp.bfloat16)
+        part[step] = gather(step).astype(jnp.bfloat16)
         soften(step + AHEAD)
 
         @pl.when(step == 0)
@@ -157,10 +150,11 @@
     @pl.loop(n - AHEAD, n - 1)
     def _(step):
         fetch_v(step).wait()
-        part[step] = gather(step, False).astype(jnp.bfloat16)
+        part[step] = gather(step).astype(jnp.bfloat16)
         dispatch(step)
 
-    seen = gather(n - 1, True)
+    fetch_v(n - 1).wait()
+    seen = gather(n - 1)
     high, total = stat[n - 1][:, 64:65], stat[n - 1][:, 0:1]
 
     def put(values):
@@ -225,7 +219,6 @@
             pltpu.SemaphoreType.DMA,
             pltpu.SemaphoreType.DMA((n,)),
             pltpu.SemaphoreType.DMA((n,)),
-            pltpu.SemaphoreType.DMA((sequences // n,)),
             pltpu.SemaphoreType.DMA((n, 2)),
             pltpu.SemaphoreType.DMA((n, 2)),
             pltpu.SemaphoreType.DMA((n,)),

time: 24.6 us -> 24.5 us (level)
  no operation moved by 1% of the time
where the time goes in v5:
time: 24.5 us
  Pallas kernels  23.8 us (97%)
  local copies, waits for them, and re-layouts  0.65 us (3%)
    pallas_call x1, Pallas kernels, attend(): pl.pallas_call(functools.partial(kernel, n), out_shape=jax.ShapeDtypeStru...  23.8 us
    reshape x1, local copies, waits for them, and re-layouts, attend(): return out.reshape(q.shape)  0.65 us

profile of v5, /device:TPU:22, one launch (start us, length us, event | category | flops | bytes accessed | tf_op | source)
XLA Modules:
  0.0 24.5 jit_solution(6488000928903624003)
XLA Ops:
  0.0 23.8 %shard_map.37 = bf16[8,16,256]{2,1,0:T(8,128)(2,1)S(1)} custom-call(bf16[32,4,256]{2,1,0:T(4,128)(2,1)} %q_hbm.1, bf16[32,1024,256]{2,1,0:T(8,128)(2,1)} %bitcast.2, bf16[32,1024,256]{2,1,0:T(8,128)(2,1)} %bitcast.3), custom_call_target="tpu_custom_call" | custom-call | tf_op jit(solution)/shard_map/pallas_call | solution.py:201
  23.8 0.7 %reshape.11 = bf16[32,4,256]{2,1,0:T(4,128)(2,1)} reshape(bf16[8,16,256]{2,1,0:T(8,128)(2,1)S(1)} %shard_map.37) | data formatting | bytes 131072 | tf_op jit(solution)/shard_map/reshape | solution.py:229

commit v6 on v5

--- a/solution.py
+++ b/solution.py
@@ -13,9 +13,13 @@
 
 
 def offset_of(step, n):
+    order = sorted(range(n), key=lambda ahead: ahead if 2 * ahead < n else n - ahead + 1.5, reverse=True)
     if isinstance(step, int):
-        return n // 2 + step if step < n // 2 else n - 1 - step
-    return jnp.where(step < n // 2, n // 2 + step, n - 1 - step)
+        return order[step]
+    offset = order[0]
+    for k in range(1, n):
+        offset = jnp.where(step == k, order[k], offset)
+    return offset
 
 
 def kernel(

time: 24.5 us -> 24.2 us (0.988)
  Pallas kernels: 23.8 us -> 23.5 us
    pallas_call x1, Pallas kernels: 23.8 us -> 23.5 us  [attend(): pl.pallas_call(functools.partial(kernel, n), out_shape=jax.ShapeDtypeStru...]
where the time goes in v6:
time: 24.2 us
  Pallas kernels  23.5 us (97%)
  local copies, waits for them, and re-layouts  0.65 us (3%)
    pallas_call x1, Pallas kernels, attend(): pl.pallas_call(functools.partial(kernel, n), out_shape=jax.ShapeDtypeStru...  23.5 us
    reshape x1, local copies, waits for them, and re-layouts, attend(): return out.reshape(q.shape)  0.65 us

profile of v6, /device:TPU:22, one launch (start us, length us, event | category | flops | bytes accessed | tf_op | source)
XLA Modules:
  0.0 24.2 jit_solution(6407855112666755768)
XLA Ops:
  0.0 23.5 %shard_map.37 = bf16[8,16,256]{2,1,0:T(8,128)(2,1)S(1)} custom-call(bf16[32,4,256]{2,1,0:T(4,128)(2,1)} %q_hbm.1, bf16[32,1024,256]{2,1,0:T(8,128)(2,1)} %bitcast.2, bf16[32,1024,256]{2,1,0:T(8,128)(2,1)} %bitcast.3), custom_call_target="tpu_custom_call" | custom-call | tf_op jit(solution)/shard_map/pallas_call | solution.py:205
  23.5 0.7 %reshape.11 = bf16[32,4,256]{2,1,0:T(4,128)(2,1)} reshape(bf16[8,16,256]{2,1,0:T(8,128)(2,1)S(1)} %shard_map.37) | data formatting | bytes 131072 | tf_op jit(solution)/shard_map/reshape | solution.py:233
